TPU v7x, 32 devices: a whole 2x2x4 slice. The times are simulated.
32 devices in a mesh: gx: 8 (over z, x), gy: 4 (over y, core).
Axes of the slice: x: 2, y: 2, z: 4, core: 2. Of those that a mesh axis runs over, the one named last changes fastest.
Arguments:
- velocity: float32 [2, 1024, 1024], P(None, 'gy', 'gx'), may hold values from -3 to 3
- stress: float32 [3, 1024, 1024], P(None, 'gy', 'gx'), may hold values from -3 to 3
- ice_mass: float32 [1024, 1024], P('gy', 'gx'), may hold values from 0.5 to 4
- strength: float32 [1024, 1024], P('gy', 'gx'), may hold values from 0.2 to 2
- land_mask: int32 [1024, 1024], P('gy', 'gx'), may hold values from 0 to 1
- ocean_forcing: float32 [4, 1024, 1024], P(None, ('gy', 'gx')), may hold values from -3 to 3
Outputs:
- velocity_out: float32 [2, 1024, 1024], P(None, 'gy', 'gx')
- stress_out: float32 [3, 1024, 1024], P(None, 'gy', 'gx')
- residuals: float32 [4], replicated
- ocean_stress: float32 [2, 1024, 1024], P(None, ('gy', 'gx'))
All inputs are finite; a program needn't handle non-finite values.
Results may differ from a plain program's by a relative error of at most 0.0001.
Values sent between devices are 32-bit elements; how exact they have to be, the bound alone decides.
A program may use at most 64 MiB of HBM per device.

v0:
```python
import jax
import jax.numpy as jnp
from jax import lax
from jax.sharding import PartitionSpec as P

ITERS = 4
ALPHA = 4.0
BETA = 4.0
WATER_DRAG = 1.0
DELTA_FLOOR = 0.0025


def extended(cells, sides, width):
    for axis, dim in sides:
        count = lax.axis_size(axis)
        head = lax.slice_in_dim(cells, 0, width, axis=dim)
        tail = lax.slice_in_dim(cells, cells.shape[dim] - width, cells.shape[dim], axis=dim)
        cells = jnp.concatenate(
            [
                lax.ppermute(tail, axis, [(i, (i + 1) % count) for i in range(count)]),
                cells,
                lax.ppermute(head, axis, [((i + 1) % count, i) for i in range(count)]),
            ],
            axis=dim,
        )
    return cells


def diff_east(padded):
    return 0.5 * (padded[..., 1:-1, 2:] - padded[..., 1:-1, :-2])


def diff_north(padded):
    return 0.5 * (padded[..., 2:, 1:-1] - padded[..., :-2, 1:-1])


def trim_edges(field, level):
    if level == 0:
        return field
    return field[..., level:-level, level:-level]


def record_sum(own_sum, global_sums):
    global_sums.append(lax.psum(own_sum, ("gx", "gy")))


def relax_stress(padded_vel, stress, strength, ice_frac):
    east_dx = diff_east(padded_vel[0])
    east_dy = diff_north(padded_vel[0])
    north_dx = diff_east(padded_vel[1])
    north_dy = diff_north(padded_vel[1])
    divergence = east_dx + north_dy
    tension = east_dx - north_dy
    shear_rate = east_dy + north_dx
    delta_rate = jnp.sqrt(
        divergence * divergence + 0.25 * (tension * tension + shear_rate * shear_rate) + DELTA_FLOOR
    )
    target = jnp.stack(
        [
            strength * (divergence / delta_rate - 1.0),
            strength * tension / (4.0 * delta_rate),
            strength * shear_rate / (8.0 * delta_rate),
        ]
    )
    return (stress + (target - stress) / ALPHA) * ice_frac


def drag_coeff(vel, currents):
    east_gap = currents[0] - vel[0]
    north_gap = currents[1] - vel[1]
    return WATER_DRAG * jnp.sqrt(east_gap * east_gap + north_gap * north_gap + 0.01)


def relax_velocity(padded_stress, vel, vel_start, forcing, ice_mass, coriolis, ice_frac):
    normal_xx = 0.5 * (padded_stress[0] + padded_stress[1])
    normal_yy = 0.5 * (padded_stress[0] - padded_stress[1])
    shear_xy = padded_stress[2]
    force_east = diff_east(normal_xx) + diff_north(shear_xy)
    force_north = diff_east(shear_xy) + diff_north(normal_yy)
    drag_rate = drag_coeff(vel, forcing[2:4])
    denominator = BETA + 1.0 + drag_rate / ice_mass
    new_east = (
        (
            BETA * vel[0]
            + vel_start[0]
            + (force_east + forcing[0] + drag_rate * forcing[2]) / ice_mass
            + coriolis * vel[1]
        )
        / denominator
        * ice_frac
    )
    new_north = (
        (
            BETA * vel[1]
            + vel_start[1]
            + (force_north + forcing[1] + drag_rate * forcing[3]) / ice_mass
            - coriolis * vel[0]
        )
        / denominator
        * ice_frac
    )
    return jnp.stack([new_east, new_north])


def local(velocity, stress, ice_mass, strength, land_mask, ocean_forcing):
    row_count = velocity.shape[1]
    col_count = velocity.shape[2]
    forcing = lax.all_to_all(ocean_forcing, "gx", split_axis=2, concat_axis=1, tiled=True)
    ice_frac = land_mask.astype(jnp.float32)
    lat_band = lax.axis_index("gy")
    total_rows = lax.axis_size("gy") * row_count
    global_sums = []
    depth = 2 * ITERS
    stacked = jnp.concatenate(
        [velocity, stress, strength[None], ice_mass[None], ice_frac[None], forcing], axis=0
    )
    padded = extended(stacked, (("gx", 2), ("gy", 1)), depth)
    wide_rows = lat_band * row_count - depth + jnp.arange(row_count + 2 * depth, dtype=jnp.int32)
    inside = ((wide_rows >= 0) & (wide_rows < total_rows)).astype(jnp.float32)[:, None]
    wide_vel = padded[0:2] * inside
    wide_stress = padded[2:5] * inside
    wide_strength = padded[5]
    wide_mass = padded[6]
    wide_ice = padded[7] * inside
    wide_forcing = padded[8:12]
    wide_lat = wide_rows.astype(jnp.float32)
    wide_coriolis = jnp.broadcast_to(
        (0.3 + 1.2 * (wide_lat + 0.5) / total_rows)[:, None],
        (row_count + 2 * depth, col_count + 2 * depth),
    )
    vel_work = wide_vel
    stress_work = wide_stress
    margin = depth
    for subcycle in range(ITERS):
        level_one = depth - (margin - 1)
        stress_cut = (stress_work.shape[-1] - (col_count + 2 * (margin - 1))) // 2
        stress_work = relax_stress(
            vel_work,
            trim_edges(stress_work, stress_cut),
            trim_edges(wide_strength, level_one),
            trim_edges(wide_ice, level_one),
        )
        level_two = depth - (margin - 2)
        old_vel = trim_edges(vel_work, 2)
        new_vel = relax_velocity(
            stress_work,
            old_vel,
            trim_edges(wide_vel, level_two),
            trim_edges(wide_forcing, level_two),
            trim_edges(wide_mass, level_two),
            trim_edges(wide_coriolis, level_two),
            trim_edges(wide_ice, level_two),
        )
        change = trim_edges(new_vel - old_vel, margin - 2)
        record_sum(jnp.sum(change * change), global_sums)
        vel_work = new_vel
        margin = margin - 2
    stress = trim_edges(stress_work, 1)
    history = jnp.stack(global_sums)
    drag_rate = drag_coeff(vel_work, forcing[2:4])
    ice_stress = drag_rate * (vel_work - forcing[2:4]) * ice_frac
    ocean_stress = lax.all_to_all(ice_stress, "gx", split_axis=1, concat_axis=2, tiled=True)
    return (vel_work, stress, history, ocean_stress)


def solution(mesh):
    placed = (
        P(None, "gy", "gx"),
        P(None, "gy", "gx"),
        P("gy", "gx"),
        P("gy", "gx"),
        P("gy", "gx"),
        P(None, ("gy", "gx"), None),
    )
    return jax.shard_map(
        local,
        mesh=mesh,
        in_specs=placed,
        out_specs=(P(None, "gy", "gx"), P(None, "gy", "gx"), P(), P(None, ("gy", "gx"), None)),
        check_vma=False,
    )
```

profile of v0, /device:TPU:0, one launch (start us, length us, event | category | flops | bytes accessed | tf_op | source)
XLA Modules:
  0.0 124.1 jit_solution(12943327118963534328)
XLA Ops:
  0.6 1.8 %copy.37 = f32[4,32,1024]{1,0,2:T(4,128)S(1)} copy(f32[4,32,1024]{2,1,0:T(8,128)} %param.11) | data formatting | bytes 1048576 | tf_op args[5]
  2.4 2.2 %reshape.95 = f32[8,1,16384]{2,1,0:T(1,128)} reshape(f32[1024,4,32]{2,1,0:T(4,128)S(1)} %bitcast.395) | data formatting | bytes 1048576
  4.6 7.4 %all-to-all-start = ((f32[8,1,16384]{2,1,0:T(1,128)}), f32[8,1,16384]{2,1,0:T(1,128)S(1)}, u32[]{:S(2)}, u32[]{:S(2)}) async-start(f32[8,1,16384]{2,1,0:T(1,128)} %reshape.95), calls=%async_computation | async-start | bytes 1048576 | tf_op jit(solution)/shard_map/all_to_all | solution.py:108
  12.2 1.0 constant_dynamic-update-slice_fusion.2
  13.5 13.0 %all-to-all-done = f32[8,1,16384]{2,1,0:T(1,128)S(1)} async-done(((f32[8,1,16384]{2,1,0:T(1,128)}), f32[8,1,16384]{2,1,0:T(1,128)S(1)}, u32[]{:S(2)}, u32[]{:S(2)}) %all-to-all-start) | async-done | bytes 524320 | tf_op jit(solution)/shard_map/all_to_all | solution.py:108
  27.0 1.9 %reduce.6 = f32[8,16384]{1,0:T(8,128)S(1)} reduce(f32[8,1,16384]{2,1,0:T(1,128)S(1)} %all-to-all-done, f32[]{:T(128)} %broadcast.256), dimensions={1}, to_apply=%all_to_all.26.reduce_sub_computation | reduce | bytes 1048580 | tf_op jit(solution)/shard_map/all_to_all | solution.py:108
  28.9 2.4 %reshape.96 = f32[1024,4,32]{2,1,0:T(4,128)} reshape(f32[8,16384]{1,0:T(8,128)S(1)} %reduce.6) | data formatting | bytes 1048576
  31.3 1.8 %copy.52 = f32[4,32,8,128]{3,1,2,0:T(8,128)S(1)} copy(f32[4,32,8,128]{1,0,3,2:T(4,128)} %bitcast.377) | data formatting | bytes 1048576 | tf_op jit(solution)/shard_map/all_to_all | solution.py:108
  33.2 1.7 %fusion.160 = (f32[12,256,8]{2,1,0:T(8,128)S(1)}, f32[12,256,8]{2,1,0:T(8,128)}) fusion(f32[12,256,128]{2,1,0:T(8,128)S(1)} %constant_dynamic-update-slice_fusion), kind=kLoop, calls=%fused_computation.288 | loop fusion | bytes 393216 | tf_op jit(solution)/shard_map/slice | solution.py:17
  34.9 1.8 %copy.41 = f32[12,256,8]{1,2,0:T(8,128)S(1)} copy(f32[12,256,8]{2,1,0:T(8,128)} %get-tuple-element.42) | data formatting | bytes 196608 | tf_op jit(solution)/shard_map/slice | solution.py:16
  36.7 2.4 %collective-permute-start.1 = (f32[12,256,8]{1,2,0:T(8,128)S(1)}, f32[12,256,8]{1,2,0:T(8,128)S(1)}, u32[]{:S(2)}, u32[]{:S(2)}) collective-permute-start(f32[12,256,8]{1,2,0:T(8,128)S(1)} %copy.41), channel_id=1, source_target_pairs={{4,0},{8,4},{12,8},{16,12},{20,16},{24,20},{28,24},{0,28},{5,1},{9... | collective-permute-start | bytes 294920 | tf_op jit(solution)/shard_map/ppermute | solution.py:22
  39.1 1.1 copy.40
  40.3 3.0 %copy.51 = f32[4,32,8,128]{3,2,1,0:T(8,128)} copy(f32[4,32,8,128]{1,0,3,2:T(4,128)} %bitcast.378) | data formatting | bytes 1048576 | tf_op jit(solution)/shard_map/all_to_all | solution.py:108
  43.8 4.1 %collective-permute-done = f32[12,256,8]{1,2,0:T(8,128)} collective-permute-done((f32[12,256,8]{1,2,0:T(8,128)}, f32[12,256,8]{1,2,0:T(8,128)}, u32[]{:S(2)}, u32[]{:S(2)}) %collective-permute-start) | collective-permute-done | bytes 98336 | tf_op jit(solution)/shard_map/ppermute | solution.py:20
  47.8 2.5 %copy.42 = f32[12,256,8]{2,1,0:T(8,128)} copy(f32[12,256,8]{1,2,0:T(8,128)} %collective-permute-done) | data formatting | bytes 196608 | tf_op jit(solution)/shard_map/ppermute | solution.py:20
  50.4 1.0 pad_maximum_fusion.7
  52.2 1.4 %collective-permute-done.3 = f32[12,8,144]{2,1,0:T(8,128)S(1)} collective-permute-done((f32[12,8,144]{2,1,0:T(8,128)S(1)}, f32[12,8,144]{2,1,0:T(8,128)S(1)}, u32[]{:S(2)}, u32[]{:S(2)}) %collective-permute-start.3) | collective-permute-done | bytes 55328 | tf_op jit(solution)/shard_map/ppermute | solution.py:22
  53.7 2.9 %collective-permute-done.2 = f32[12,8,144]{2,1,0:T(8,128)S(1)} collective-permute-done((f32[12,8,144]{2,1,0:T(8,128)S(1)}, f32[12,8,144]{2,1,0:T(8,128)S(1)}, u32[]{:S(2)}, u32[]{:S(2)}) %collective-permute-start.2) | collective-permute-done | bytes 55328 | tf_op jit(solution)/shard_map/ppermute | solution.py:20
  56.6 1.3 %pad_maximum_fusion = f32[12,272,144]{2,1,0:T(8,128)S(1)} fusion(f32[12,8,144]{2,1,0:T(8,128)S(1)} %collective-permute-done.3, f32[12,256,8]{2,1,0:T(8,128)S(1)} %copy.43, f32[12,256,128]{2,1,0:T(8,128)S(1)} %constant_dynamic-update-slice_fusion, f32[12,256,8]{2,1,0:T(8,128)S(1)} %copy-done.2, f32[12,8,144]{2,1,0:T(8,128)S(1)} %collective-permute-done.2), kind=kLoop, calls=%fused_computation | loop fusion | flops 1880064 | bytes 3760128 | tf_op jit(solution)/shard_map/concatenate | solution.py:18
  58.7 0.9 copy-done
  61.9 1.5 %copy-done.1 = f32[12,272,144]{2,1,0:T(8,128)S(1)} copy-done((f32[12,272,144]{2,1,0:T(8,128)S(1)}, f32[12,272,144]{2,1,0:T(8,128)}, u32[]{:S(2)}) %copy-start.1) | copy-done | bytes 1880088
  63.4 0.9 fusion.19
  66.4 0.9 fusion.71
  67.3 0.9 fusion.83
  69.5 0.9 fusion.48
  70.4 0.9 fusion.59
  73.4 0.9 copy.49
  74.3 3.4 %all-to-all-start.1 = ((f32[2,256,128]{2,0,1:T(2,128)}), f32[2,256,128]{2,0,1:T(2,128)S(1)}, u32[]{:S(2)}, u32[]{:S(2)}) async-start(f32[2,256,128]{2,0,1:T(2,128)} %copy.49), calls=%async_computation.1 | async-start | bytes 524288 | tf_op jit(solution)/shard_map/all_to_all | solution.py:162
  78.0 1.2 fusion.98
  79.2 40.1 %all-reduce = (f32[1]{0:T(128)}, f32[1]{0:T(128)}, f32[1]{0:T(128)}, f32[1]{0:T(128)}) all-reduce(f32[1]{0:T(128)} %bitcast.78, f32[1]{0:T(128)} %bitcast.77, f32[1]{0:T(128)} %bitcast.76, f32[1]{0:T(128)} %bitcast.75), channel_id=1, replica_groups=mesh['gx'=8,'gy'=4] {'gx','gy'}, use_global_device_ids=true, to_apply=%region_7.0 | all-reduce | flops 4 | bytes 32 | tf_op jit(solution)/shard_map/psum | solution.py:44
  119.3 0.9 slice.886
  120.2 3.0 %pad_maximum_fusion.8 = f32[4]{0:T(128)} fusion(f32[1]{0:T(128)} %get-tuple-element.12, f32[1]{0:T(128)} %get-tuple-element.13, f32[1]{0:T(128)} %get-tuple-element.14, f32[1]{0:T(128)} %get-tuple-element.15), kind=kLoop, calls=%fused_computation.287 | loop fusion | flops 12 | bytes 32 | tf_op jit(solution)/shard_map/stack | solution.py:159
  (74 shorter events, 11.8 us)
Async XLA Ops:
  2.4 9.8 %copy-start.5 = (s32[256,128]{1,0:T(8,128)S(1)}, s32[256,128]{1,0:T(8,128)}, u32[]{:S(2)}) copy-start(s32[256,128]{1,0:T(8,128)} %param.10) | copy-start | bytes 393220
  4.6 8.8 %copy-start.6 = (f32[3,256,128]{2,1,0:T(8,128)S(1)}, f32[3,256,128]{2,1,0:T(8,128)}, u32[]{:S(2)}) copy-start(f32[3,256,128]{2,1,0:T(8,128)} %param.7) | copy-start | bytes 1179652
  4.6 8.8 %copy-start.7 = (f32[256,128]{1,0:T(8,128)S(1)}, f32[256,128]{1,0:T(8,128)}, u32[]{:S(2)}) copy-start(f32[256,128]{1,0:T(8,128)} %param.9) | copy-start | bytes 393220
  4.6 8.8 %copy-start.8 = (f32[256,128]{1,0:T(8,128)S(1)}, f32[256,128]{1,0:T(8,128)}, u32[]{:S(2)}) copy-start(f32[256,128]{1,0:T(8,128)} %param.8) | copy-start | bytes 393220
  4.6 21.9 %all-to-all-start = ((f32[8,1,16384]{2,1,0:T(1,128)}), f32[8,1,16384]{2,1,0:T(1,128)S(1)}, u32[]{:S(2)}, u32[]{:S(2)}) async-start(f32[8,1,16384]{2,1,0:T(1,128)} %reshape.95), calls=%async_computation | async-start | bytes 1048576 | tf_op jit(solution)/shard_map/all_to_all | solution.py:108
  36.7 6.5 %collective-permute-start.1 = (f32[12,256,8]{1,2,0:T(8,128)S(1)}, f32[12,256,8]{1,2,0:T(8,128)S(1)}, u32[]{:S(2)}, u32[]{:S(2)}) collective-permute-start(f32[12,256,8]{1,2,0:T(8,128)S(1)} %copy.41), channel_id=1, source_target_pairs={{4,0},{8,4},{12,8},{16,12},{20,16},{24,20},{28,24},{0,28},{5,1},{9... | collective-permute-start | bytes 294920 | tf_op jit(solution)/shard_map/ppermute | solution.py:22
  40.2 7.6 %collective-permute-start = (f32[12,256,8]{1,2,0:T(8,128)}, f32[12,256,8]{1,2,0:T(8,128)}, u32[]{:S(2)}, u32[]{:S(2)}) collective-permute-start(f32[12,256,8]{1,2,0:T(8,128)} %copy.40), channel_id=1, source_target_pairs={{0,4},{4,8},{8,12},{12,16},{16,20},{20,24},{24,28},{28,0},{1,5},{5... | collective-permute-start | bytes 294920 | tf_op jit(solution)/shard_map/ppermute | solution.py:20
  50.4 1.6 %copy-start.3 = (f32[4,32,8,128]{3,2,1,0:T(8,128)S(1)}, f32[4,32,8,128]{3,2,1,0:T(8,128)}, u32[]{:S(2)}) copy-start(f32[4,32,8,128]{3,2,1,0:T(8,128)} %copy.51) | copy-start | bytes 1572868
  51.4 2.3 %collective-permute-start.3 = (f32[12,8,144]{2,1,0:T(8,128)S(1)}, f32[12,8,144]{2,1,0:T(8,128)S(1)}, u32[]{:S(2)}, u32[]{:S(2)}) collective-permute-start(f32[12,8,144]{2,1,0:T(8,128)S(1)} %get-tuple-element.38), channel_id=1, source_target_pairs={{1,0},{2,1},{3,2},{0,3},{5,4},{6,5},{7,6},{4,7},{9,8},{10,9},{11,1... | collective-permute-start | bytes 165896 | tf_op jit(solution)/shard_map/ppermute | solution.py:22
  51.5 5.2 %collective-permute-start.2 = (f32[12,8,144]{2,1,0:T(8,128)S(1)}, f32[12,8,144]{2,1,0:T(8,128)S(1)}, u32[]{:S(2)}, u32[]{:S(2)}) collective-permute-start(f32[12,8,144]{2,1,0:T(8,128)S(1)} %get-tuple-element.37), channel_id=1, source_target_pairs={{0,1},{1,2},{2,3},{3,0},{4,5},{5,6},{6,7},{7,4},{8,9},{9,10},{10,1... | collective-permute-start | bytes 165896 | tf_op jit(solution)/shard_map/ppermute | solution.py:20
  52.0 4.7 %copy-start.2 = (f32[12,256,8]{2,1,0:T(8,128)S(1)}, f32[12,256,8]{2,1,0:T(8,128)}, u32[]{:S(2)}) copy-start(f32[12,256,8]{2,1,0:T(8,128)} %copy.42) | copy-start | bytes 294916
  57.9 1.7 %copy-start = (f32[12,272,144]{2,1,0:T(8,128)}, f32[12,272,144]{2,1,0:T(8,128)S(1)}, u32[]{:S(2)}) copy-start(f32[12,272,144]{2,1,0:T(8,128)S(1)} %pad_maximum_fusion) | copy-start | bytes 5640196
  60.3 1.2 slice-start
  61.5 1.9 %copy-start.1 = (f32[12,272,144]{2,1,0:T(8,128)S(1)}, f32[12,272,144]{2,1,0:T(8,128)}, u32[]{:S(2)}) copy-start(f32[12,272,144]{2,1,0:T(8,128)} %copy-done) | copy-start | bytes 5640196
  73.4 5.7 %copy-start.4 = (f32[2,256,128]{2,1,0:T(8,128)}, f32[2,256,128]{2,1,0:T(8,128)S(1)}, u32[]{:S(2)}) copy-start(f32[2,256,128]{2,1,0:T(8,128)S(1)} %get-tuple-element.17) | copy-start | bytes 786436
  74.3 48.9 %all-to-all-start.1 = ((f32[2,256,128]{2,0,1:T(2,128)}), f32[2,256,128]{2,0,1:T(2,128)S(1)}, u32[]{:S(2)}, u32[]{:S(2)}) async-start(f32[2,256,128]{2,0,1:T(2,128)} %copy.49), calls=%async_computation.1 | async-start | bytes 524288 | tf_op jit(solution)/shard_map/all_to_all | solution.py:162
where the time goes:
time: 125 us; the launch traced here: 124 us
  blocking collectives  40.1 us (32%)
  local copies, waits for them, and re-layouts  27.9 us (22%)
  waiting for transfers between devices  21.5 us (17%)
  other arithmetic  19.8 us (16%)
  starting transfers between devices  13.8 us (11%)
    psum x1, blocking collectives, record_sum(): global_sums.append(lax.psum(own_sum, ('gx', 'gy')))  40.1 us
    all_to_all x1, waiting for transfers between devices, local(): lax.all_to_all(ocean_forcing, 'gx', split_axis=2, concat_axis=1, tiled=True)  13 us
    unnamed x25, local copies, waits for them, and re-layouts  9.82 us
    all_to_all x1, starting transfers between devices, local(): lax.all_to_all(ocean_forcing, 'gx', split_axis=2, concat_axis=1, tiled=True)  7.41 us
    ppermute x2, waiting for transfers between devices, extended(): lax.ppermute(tail, axis, [(i, (i + 1) % count) for i in range(count)])  7.03 us
    all_to_all x3, local copies, waits for them, and re-layouts, local(): lax.all_to_all(ocean_forcing, 'gx', split_axis=2, concat_axis=1, tiled=True)  5.33 us
    another operation x8, other arithmetic, relax_stress(): jnp.stack([strength * (divergence / delta_rate - 1.0), strength * tension...  3.65 us
    all_to_all x1, starting transfers between devices, local(): lax.all_to_all(ice_stress, 'gx', split_axis=1, concat_axis=2, tiled=True)  3.41 us
  transfers between devices with their start and end apart: 6, of which 4 were waited for; matrix products, arithmetic and copies ran while one was open for 9% of the time, Pallas kernels for 0%

commit v1 on v0

--- a/solution.py
+++ b/solution.py
@@ -41,7 +41,7 @@
 
 
 def record_sum(own_sum, global_sums):
-    global_sums.append(lax.psum(own_sum, ("gx", "gy")))
+    global_sums.append(jnp.sum(lax.all_gather(own_sum, ("gx", "gy")), axis=0))
 
 
 def relax_stress(padded_vel, stress, strength, ice_frac):

time: 125 us -> 130 us (1.040)
  local copies, waits for them, and re-layouts: 27.9 us -> 30.8 us
  other arithmetic: 19.8 us -> 22.3 us
    psum x1 -> x0, blocking collectives: 40.1 us -> none  [record_sum(): global_sums.append(lax.psum(own_sum, ('gx', 'gy')))]
    unnamed x0 -> x1, blocking collectives: none -> 39.8 us
    unnamed x25 -> x33, local copies, waits for them, and re-layouts: 9.82 us -> 12.7 us
    reduce_sum x0 -> x4, other arithmetic: none -> 2.51 us  [record_sum(): global_sums.append(jnp.sum(lax.all_gather(own_sum, ('gx', 'gy')), axis=0))]
  transfers between devices with their start and end apart: 6 -> 6, of which waited for: 4 -> 4; matrix products, arithmetic and copies ran while one was open for 9% -> 13% of each run, Pallas kernels for 0% -> 0%
where the time goes in v1:
time: 130 us; the launch traced here: 129 us
  blocking collectives  39.8 us (31%)
  local copies, waits for them, and re-layouts  30.8 us (24%)
  other arithmetic  22.3 us (17%)
  waiting for transfers between devices  21.5 us (17%)
  starting transfers between devices  13.8 us (11%)
    unnamed x1, blocking collectives  39.8 us
    all_to_all x1, waiting for transfers between devices, local(): lax.all_to_all(ocean_forcing, 'gx', split_axis=2, concat_axis=1, tiled=True)  13 us
    unnamed x33, local copies, waits for them, and re-layouts  12.7 us
    all_to_all x1, starting transfers between devices, local(): lax.all_to_all(ocean_forcing, 'gx', split_axis=2, concat_axis=1, tiled=True)  7.41 us
    ppermute x2, waiting for transfers between devices, extended(): lax.ppermute(tail, axis, [(i, (i + 1) % count) for i in range(count)])  7.05 us
    all_to_all x3, local copies, waits for them, and re-layouts, local(): lax.all_to_all(ocean_forcing, 'gx', split_axis=2, concat_axis=1, tiled=True)  5.32 us
    another operation x8, other arithmetic, relax_stress(): jnp.stack([strength * (divergence / delta_rate - 1.0), strength * tension...  3.65 us
    all_to_all x1, starting transfers between devices, local(): lax.all_to_all(ice_stress, 'gx', split_axis=1, concat_axis=2, tiled=True)  3.41 us
  transfers between devices with their start and end apart: 6, of which 4 were waited for; matrix products, arithmetic and copies ran while one was open for 13% of the time, Pallas kernels for 0%

profile of v1, /device:TPU:0, one launch (start us, length us, event | category | flops | bytes accessed | tf_op | source)
XLA Modules:
  0.0 129.2 jit_solution(6858294272316270593)
XLA Ops:
  0.6 1.8 %copy.37 = f32[4,32,1024]{1,0,2:T(4,128)S(1)} copy(f32[4,32,1024]{2,1,0:T(8,128)} %param.11) | data formatting | bytes 1048576 | tf_op args[5]
  2.4 2.1 %reshape.103 = f32[8,1,16384]{2,1,0:T(1,128)} reshape(f32[1024,4,32]{2,1,0:T(4,128)S(1)} %bitcast.399) | data formatting | bytes 1048576
  4.6 7.4 %all-to-all-start = ((f32[8,1,16384]{2,1,0:T(1,128)}), f32[8,1,16384]{2,1,0:T(1,128)S(1)}, u32[]{:S(2)}, u32[]{:S(2)}) async-start(f32[8,1,16384]{2,1,0:T(1,128)} %reshape.103), calls=%async_computation | async-start | bytes 1048576 | tf_op jit(solution)/shard_map/all_to_all | solution.py:108
  12.2 1.0 constant_dynamic-update-slice_fusion.2
  13.4 13.0 %all-to-all-done = f32[8,1,16384]{2,1,0:T(1,128)S(1)} async-done(((f32[8,1,16384]{2,1,0:T(1,128)}), f32[8,1,16384]{2,1,0:T(1,128)S(1)}, u32[]{:S(2)}, u32[]{:S(2)}) %all-to-all-start) | async-done | bytes 524320 | tf_op jit(solution)/shard_map/all_to_all | solution.py:108
  27.0 1.9 %reduce.10 = f32[8,16384]{1,0:T(8,128)S(1)} reduce(f32[8,1,16384]{2,1,0:T(1,128)S(1)} %all-to-all-done, f32[]{:T(128)} %broadcast.260), dimensions={1}, to_apply=%all_to_all.26.reduce_sub_computation | reduce | bytes 1048580 | tf_op jit(solution)/shard_map/all_to_all | solution.py:108
  28.9 2.4 %reshape.104 = f32[1024,4,32]{2,1,0:T(4,128)} reshape(f32[8,16384]{1,0:T(8,128)S(1)} %reduce.10) | data formatting | bytes 1048576
  31.3 1.8 %copy.52 = f32[4,32,8,128]{3,1,2,0:T(8,128)S(1)} copy(f32[4,32,8,128]{1,0,3,2:T(4,128)} %bitcast.381) | data formatting | bytes 1048576 | tf_op jit(solution)/shard_map/all_to_all | solution.py:108
  33.2 1.7 %fusion.160 = (f32[12,256,8]{2,1,0:T(8,128)S(1)}, f32[12,256,8]{2,1,0:T(8,128)}) fusion(f32[12,256,128]{2,1,0:T(8,128)S(1)} %constant_dynamic-update-slice_fusion), kind=kLoop, calls=%fused_computation.288 | loop fusion | bytes 393216 | tf_op jit(solution)/shard_map/slice | solution.py:17
  34.9 1.8 %copy.41 = f32[12,256,8]{1,2,0:T(8,128)S(1)} copy(f32[12,256,8]{2,1,0:T(8,128)} %get-tuple-element.42) | data formatting | bytes 196608 | tf_op jit(solution)/shard_map/slice | solution.py:16
  36.7 2.4 %collective-permute-start.1 = (f32[12,256,8]{1,2,0:T(8,128)S(1)}, f32[12,256,8]{1,2,0:T(8,128)S(1)}, u32[]{:S(2)}, u32[]{:S(2)}) collective-permute-start(f32[12,256,8]{1,2,0:T(8,128)S(1)} %copy.41), channel_id=1, source_target_pairs={{4,0},{8,4},{12,8},{16,12},{20,16},{24,20},{28,24},{0,28},{5,1},{9... | collective-permute-start | bytes 294920 | tf_op jit(solution)/shard_map/ppermute | solution.py:22
  39.1 1.1 copy.40
  40.3 3.0 %copy.51 = f32[4,32,8,128]{3,2,1,0:T(8,128)} copy(f32[4,32,8,128]{1,0,3,2:T(4,128)} %bitcast.382) | data formatting | bytes 1048576 | tf_op jit(solution)/shard_map/all_to_all | solution.py:108
  43.7 4.1 %collective-permute-done = f32[12,256,8]{1,2,0:T(8,128)} collective-permute-done((f32[12,256,8]{1,2,0:T(8,128)}, f32[12,256,8]{1,2,0:T(8,128)}, u32[]{:S(2)}, u32[]{:S(2)}) %collective-permute-start) | collective-permute-done | bytes 98336 | tf_op jit(solution)/shard_map/ppermute | solution.py:20
  47.8 2.5 %copy.42 = f32[12,256,8]{2,1,0:T(8,128)} copy(f32[12,256,8]{1,2,0:T(8,128)} %collective-permute-done) | data formatting | bytes 196608 | tf_op jit(solution)/shard_map/ppermute | solution.py:20
  50.4 1.0 pad_maximum_fusion.7
  52.2 1.4 %collective-permute-done.3 = f32[12,8,144]{2,1,0:T(8,128)S(1)} collective-permute-done((f32[12,8,144]{2,1,0:T(8,128)S(1)}, f32[12,8,144]{2,1,0:T(8,128)S(1)}, u32[]{:S(2)}, u32[]{:S(2)}) %collective-permute-start.3) | collective-permute-done | bytes 55328 | tf_op jit(solution)/shard_map/ppermute | solution.py:22
  53.7 2.9 %collective-permute-done.2 = f32[12,8,144]{2,1,0:T(8,128)S(1)} collective-permute-done((f32[12,8,144]{2,1,0:T(8,128)S(1)}, f32[12,8,144]{2,1,0:T(8,128)S(1)}, u32[]{:S(2)}, u32[]{:S(2)}) %collective-permute-start.2) | collective-permute-done | bytes 55328 | tf_op jit(solution)/shard_map/ppermute | solution.py:20
  56.6 1.3 pad_maximum_fusion
  58.7 0.9 copy-done
  61.8 1.5 %copy-done.1 = f32[12,272,144]{2,1,0:T(8,128)S(1)} copy-done((f32[12,272,144]{2,1,0:T(8,128)S(1)}, f32[12,272,144]{2,1,0:T(8,128)}, u32[]{:S(2)}) %copy-start.1) | copy-done | bytes 1880088
  63.4 0.9 fusion.19
  66.4 0.9 fusion.71
  67.3 0.9 fusion.83
  69.5 0.9 fusion.48
  70.4 0.9 fusion.59
  73.4 0.9 copy.49
  74.3 3.4 %all-to-all-start.1 = ((f32[2,256,128]{2,0,1:T(2,128)}), f32[2,256,128]{2,0,1:T(2,128)S(1)}, u32[]{:S(2)}, u32[]{:S(2)}) async-start(f32[2,256,128]{2,0,1:T(2,128)} %copy.49), calls=%async_computation.1 | async-start | bytes 524288 | tf_op jit(solution)/shard_map/all_to_all | solution.py:162
  77.9 1.2 fusion.98
  82.1 39.8 %all-reduce.4 = (f32[32]{0:T(128)S(1)}, f32[32]{0:T(128)S(1)}, f32[32]{0:T(128)S(1)}, f32[32]{0:T(128)S(1)}) all-reduce(f32[32]{0:T(128)S(1)} %dynamic-update-slice.3, f32[32]{0:T(128)S(1)} %dynamic-update-slice.2, f32[32]{0:T(128)S(1)} %dynamic-update-slice.1, f32[32]{0:T(128)S(1)} %dynamic-update-slice), channel_id=1, replica_groups=mesh['gx'=8,'gy'=4] {'gx','gy'}, use_global_device_ids=true, to_apply=%add.3 | all-reduce | flops 128 | bytes 1024
  121.8 0.9 slice.886
  125.2 3.0 %pad_maximum_fusion.8 = f32[4]{0:T(128)} fusion(f32[1]{0:T(128)} %bitcast.82, f32[1]{0:T(128)} %bitcast.80, f32[1]{0:T(128)} %bitcast.78, f32[1]{0:T(128)} %bitcast.76), kind=kLoop, calls=%fused_computation.287 | loop fusion | flops 12 | bytes 32 | tf_op jit(solution)/shard_map/stack | solution.py:159
  (86 shorter events, 17.2 us)
Async XLA Ops:
  2.4 9.8 %copy-start.5 = (s32[256,128]{1,0:T(8,128)S(1)}, s32[256,128]{1,0:T(8,128)}, u32[]{:S(2)}) copy-start(s32[256,128]{1,0:T(8,128)} %param.10) | copy-start | bytes 393220
  4.5 8.8 %copy-start.6 = (f32[3,256,128]{2,1,0:T(8,128)S(1)}, f32[3,256,128]{2,1,0:T(8,128)}, u32[]{:S(2)}) copy-start(f32[3,256,128]{2,1,0:T(8,128)} %param.7) | copy-start | bytes 1179652
  4.5 8.8 %copy-start.7 = (f32[256,128]{1,0:T(8,128)S(1)}, f32[256,128]{1,0:T(8,128)}, u32[]{:S(2)}) copy-start(f32[256,128]{1,0:T(8,128)} %param.9) | copy-start | bytes 393220
  4.5 8.8 %copy-start.8 = (f32[256,128]{1,0:T(8,128)S(1)}, f32[256,128]{1,0:T(8,128)}, u32[]{:S(2)}) copy-start(f32[256,128]{1,0:T(8,128)} %param.8) | copy-start | bytes 393220
  4.6 21.9 %all-to-all-start = ((f32[8,1,16384]{2,1,0:T(1,128)}), f32[8,1,16384]{2,1,0:T(1,128)S(1)}, u32[]{:S(2)}, u32[]{:S(2)}) async-start(f32[8,1,16384]{2,1,0:T(1,128)} %reshape.103), calls=%async_computation | async-start | bytes 1048576 | tf_op jit(solution)/shard_map/all_to_all | solution.py:108
  36.7 6.5 %collective-permute-start.1 = (f32[12,256,8]{1,2,0:T(8,128)S(1)}, f32[12,256,8]{1,2,0:T(8,128)S(1)}, u32[]{:S(2)}, u32[]{:S(2)}) collective-permute-start(f32[12,256,8]{1,2,0:T(8,128)S(1)} %copy.41), channel_id=1, source_target_pairs={{4,0},{8,4},{12,8},{16,12},{20,16},{24,20},{28,24},{0,28},{5,1},{9... | collective-permute-start | bytes 294920 | tf_op jit(solution)/shard_map/ppermute | solution.py:22
  40.2 7.6 %collective-permute-start = (f32[12,256,8]{1,2,0:T(8,128)}, f32[12,256,8]{1,2,0:T(8,128)}, u32[]{:S(2)}, u32[]{:S(2)}) collective-permute-start(f32[12,256,8]{1,2,0:T(8,128)} %copy.40), channel_id=1, source_target_pairs={{0,4},{4,8},{8,12},{12,16},{16,20},{20,24},{24,28},{28,0},{1,5},{5... | collective-permute-start | bytes 294920 | tf_op jit(solution)/shard_map/ppermute | solution.py:20
  50.3 1.6 %copy-start.3 = (f32[4,32,8,128]{3,2,1,0:T(8,128)S(1)}, f32[4,32,8,128]{3,2,1,0:T(8,128)}, u32[]{:S(2)}) copy-start(f32[4,32,8,128]{3,2,1,0:T(8,128)} %copy.51) | copy-start | bytes 1572868
  51.4 2.3 %collective-permute-start.3 = (f32[12,8,144]{2,1,0:T(8,128)S(1)}, f32[12,8,144]{2,1,0:T(8,128)S(1)}, u32[]{:S(2)}, u32[]{:S(2)}) collective-permute-start(f32[12,8,144]{2,1,0:T(8,128)S(1)} %get-tuple-element.38), channel_id=1, source_target_pairs={{1,0},{2,1},{3,2},{0,3},{5,4},{6,5},{7,6},{4,7},{9,8},{10,9},{11,1... | collective-permute-start | bytes 165896 | tf_op jit(solution)/shard_map/ppermute | solution.py:22
  51.4 5.2 %collective-permute-start.2 = (f32[12,8,144]{2,1,0:T(8,128)S(1)}, f32[12,8,144]{2,1,0:T(8,128)S(1)}, u32[]{:S(2)}, u32[]{:S(2)}) collective-permute-start(f32[12,8,144]{2,1,0:T(8,128)S(1)} %get-tuple-element.37), channel_id=1, source_target_pairs={{0,1},{1,2},{2,3},{3,0},{4,5},{5,6},{6,7},{7,4},{8,9},{9,10},{10,1... | collective-permute-start | bytes 165896 | tf_op jit(solution)/shard_map/ppermute | solution.py:20
  51.9 4.7 %copy-start.2 = (f32[12,256,8]{2,1,0:T(8,128)S(1)}, f32[12,256,8]{2,1,0:T(8,128)}, u32[]{:S(2)}) copy-start(f32[12,256,8]{2,1,0:T(8,128)} %copy.42) | copy-start | bytes 294916
  57.9 1.7 %copy-start = (f32[12,272,144]{2,1,0:T(8,128)}, f32[12,272,144]{2,1,0:T(8,128)S(1)}, u32[]{:S(2)}) copy-start(f32[12,272,144]{2,1,0:T(8,128)S(1)} %pad_maximum_fusion) | copy-start | bytes 5640196
  60.3 1.2 slice-start
  61.4 1.9 %copy-start.1 = (f32[12,272,144]{2,1,0:T(8,128)S(1)}, f32[12,272,144]{2,1,0:T(8,128)}, u32[]{:S(2)}) copy-start(f32[12,272,144]{2,1,0:T(8,128)} %copy-done) | copy-start | bytes 5640196
  73.4 5.8 %copy-start.4 = (f32[2,256,128]{2,1,0:T(8,128)}, f32[2,256,128]{2,1,0:T(8,128)S(1)}, u32[]{:S(2)}) copy-start(f32[2,256,128]{2,1,0:T(8,128)S(1)} %get-tuple-element.17) | copy-start | bytes 786436
  74.3 54.0 %all-to-all-start.1 = ((f32[2,256,128]{2,0,1:T(2,128)}), f32[2,256,128]{2,0,1:T(2,128)S(1)}, u32[]{:S(2)}, u32[]{:S(2)}) async-start(f32[2,256,128]{2,0,1:T(2,128)} %copy.49), calls=%async_computation.1 | async-start | bytes 524288 | tf_op jit(solution)/shard_map/all_to_all | solution.py:162
